TPU v7x, 32 devices: a whole 2x2x4 slice. The times are simulated.
32 devices in a mesh: groups: 2 (over y), feat: 4 (over x, core), loop: 4 (over z).
Axes of the slice: x: 2, y: 2, z: 4, core: 2. Of those that a mesh axis runs over, the one named last changes fastest.
Arguments:
- train_grads: bfloat16 [512, 65536], P(('groups', 'loop'), 'feat'), parts along dimension 0, may hold values from -6 to 6
- query_grads: bfloat16 [64, 65536], P(('groups', 'loop'), 'feat'), parts along dimension 0, may hold values from -0.0234375 to 0.0234375
- curvature: float32 [65536], P('feat'), may hold values from 0.05 to 5
- row_counts: int32 [8], P(('groups', 'loop')), parts along dimension 0, may hold values from 1 to 64, 128 in all
Outputs:
- scores: float32 [512, 32], P(('groups', 'loop', 'feat')), parts along dimension 0
There are 2 independent parts, one for each index of `groups`. A program takes and returns all parts, laid end to end along the dimension named above; an argument that names none is the same for every part. Nothing has to cross between parts.
Inputs may be any that keep to these rules, and one draw needn't show every extreme that they name: row_counts[s] is the number of live slots of loop shard s; slots 0 to row_counts[s] - 1 of that shard are live; some shard has exactly 64; the counts sum to 128.
All inputs are finite; a program needn't handle non-finite values.
Results may differ from a plain program's by a relative error of at most 0.0029.
Values may be sent and summed in bfloat16 or wider, within the bound.
A program may use at most 128 MiB of HBM per device.

v0:
```python
import jax
import jax.numpy as jnp
from jax import lax
from jax.sharding import PartitionSpec as P

damping_term = 0.1


def scale_rows(block, curvature):
    return (block.astype(jnp.float32) / (damping_term + curvature[None, :])).astype(jnp.bfloat16)


def product(rows, piece):
    return lax.dot_general(
        rows, piece, (((1,), (1,)), ((), ())), preferred_element_type=jnp.float32
    )


def on_device(train_grads, query_grads, curvature, row_counts):
    slots = train_grads.shape[0]
    live_count = row_counts[0]
    live = (jnp.arange(slots, dtype=jnp.int32) < live_count)[:, None]
    scaled = scale_rows(lax.all_gather(query_grads, "loop", axis=0, tiled=True), curvature)
    raw = product(train_grads, scaled)
    partial_scores = jnp.where(live, raw, jnp.float32(0.0))
    return lax.psum_scatter(partial_scores, "feat", scatter_dimension=0, tiled=True)


def solution(mesh):
    placed = (
        P(("groups", "loop"), "feat"),
        P(("groups", "loop"), "feat"),
        P("feat"),
        P(("groups", "loop")),
    )
    return jax.shard_map(
        on_device,
        mesh=mesh,
        in_specs=placed,
        out_specs=P(("groups", "loop", "feat"), None),
        check_vma=False,
    )
```

profile of v0, /device:TPU:0, one launch (start us, length us, event | category | flops | bytes accessed | tf_op | source)
XLA Modules:
  0.0 68.1 jit_solution(11935903031484605481)
XLA Ops:
  6.5 0.0 copy-start
  6.5 0.0 all-gather.2.cloned.1.call-start
  6.5 0.7 %all-gather.2.cloned.1.call-update = ((bf16[8,16384]{1,0:T(8,128)(2,1)}), bf16[32,16384]{1,0:T(8,128)(2,1)}) async-update(((), (), s32[]{:S(2)}) %all-gather.2.cloned.1.call-start, bf16[8,16384]{1,0:T(8,128)(2,1)} %param.5) | async-update | bytes 1572888
  7.3 0.0 reduce-scatter.4.cloned.1.call-start
  8.0 0.8 %broadcast_add_fusion = f32[16384]{0:T(1024)S(1)} fusion(f32[16384]{0:T(1024)} %param.6), kind=kLoop, calls=%fused_computation.3 | loop fusion | flops 16384 | bytes 131072 | tf_op jit(solution)/shard_map/add | solution.py:10
  8.8 30.8 %all-gather.2.cloned.1.call-done = bf16[32,16384]{1,0:T(8,128)(2,1)} async-done(((bf16[8,16384]{1,0:T(8,128)(2,1)}), bf16[32,16384]{1,0:T(8,128)(2,1)}) %all-gather.2.cloned.1.call-update) | async-done | bytes 1048592 | tf_op jit(solution)/shard_map/all_gather | solution.py:23
  39.6 0.0 copy-done
  39.6 1.9 %fusion = f32[64,32]{0,1:T(8,128)S(1)} fusion(bf16[64,16384]{1,0:T(8,128)(2,1)S(1)} %copy-done, bf16[32,16384]{1,0:T(8,128)(2,1)} %all-gather.2.cloned.1.call-done, f32[16384]{0:T(1024)S(1)} %broadcast_add_fusion, pred[64]{0:T(512)(128)(4,1)S(1)} %iota_compare_fusion), kind=kOutput, calls=%fused_computation.2 | convolution fusion | flops 68683776 | bytes 3219520 | tf_op jit(solution)/shard_map/dot_general | solution.py:14
  41.5 0.7 %copy.7 = f32[64,32]{1,0:T(8,128)} copy(f32[64,32]{0,1:T(8,128)S(1)} %fusion) | data formatting | bytes 16384
  42.2 0.0 reduce-scatter.4.cloned.1.call-update
  42.3 19.0 %reduce-scatter.4.cloned.1.call-done = f32[16,32]{1,0:T(8,128)} async-done(((f32[64,32]{1,0:T(8,128)}), f32[16,32]{1,0:T(8,128)}) %reduce-scatter.4.cloned.1.call-update) | async-done | bytes 2064 | tf_op jit(solution)/shard_map/reduce_scatter | solution.py:26
  (1 shorter events, 0.0 us)
Async XLA Ops:
  6.5 33.1 %copy-start = (bf16[64,16384]{1,0:T(8,128)(2,1)S(1)}, bf16[64,16384]{1,0:T(8,128)(2,1)}, u32[]{:S(2)}) copy-start(bf16[64,16384]{1,0:T(8,128)(2,1)} %param.4) | copy-start | bytes 6291460
  6.5 33.1 %all-gather.2.cloned.1.call-start = ((), (), s32[]{:S(2)}) async-start(), calls=%async_computation.1 | async-start | bytes 1310720 | tf_op jit(solution)/shard_map/all_gather | solution.py:23
  7.3 54.0 %reduce-scatter.4.cloned.1.call-start = ((), (), s32[]{:S(2)}) async-start(), calls=%async_computation.2 | async-start | bytes 40960 | tf_op jit(solution)/shard_map/reduce_scatter | solution.py:26
Sparse Core Ops, SparseCore 0:
  8.9 30.6 all-gather.1
  42.4 18.8 reduce-scatter.3
where the time goes:
time: 68.3 us; the launch traced here: 68.1 us
  waiting for transfers between devices  50.6 us (74%)
  between operations  14.1 us (21%)
  matrix products  1.88 us (3%)
  other arithmetic  0.86 us (1%)
  local copies, waits for them, and re-layouts  0.7 us (1%)
    all_gather x1, waiting for transfers between devices, on_device(): lax.all_gather(query_grads, 'loop', axis=0, tiled=True)  30.8 us
    reduce_scatter x1, waiting for transfers between devices, on_device(): lax.psum_scatter(partial_scores, 'feat', scatter_dimension=0, tiled=True)  19 us
    dot_general x1, matrix products, product(): lax.dot_general(rows, piece, (((1,), (1,)), ((), ())), preferred_element_...  1.88 us
  transfers between devices with their start and end apart: 2, of which 2 were waited for; matrix products, arithmetic and copies ran while one was open for 1% of the time, Pallas kernels for 0%

commit v1 on v0

v1 whole, which is shorter than its diff:
```python
import functools

import jax
import jax.numpy as jnp
from jax import lax
from jax.experimental import pallas as pl
from jax.experimental.pallas import tpu as pltpu
from jax.sharding import PartitionSpec as P

MESH = pl.DeviceIdType.MESH
damping_term = 0.1


def kernel(
    n, nf, pieces,
    t_hbm, q_hbm, c_hbm, count_hbm, out_ref,
    gath, t_ref, count_ref, c_ref, inv_ref, acc, part, red,
    local_sem, recv_sem, send_sem, red_recv, red_send,
):
    me, f = lax.axis_index("loop"), lax.axis_index("feat")
    rows, width = t_ref.shape
    own_rows = rows // nf
    q_rows = gath.shape[1]
    cols = width // pieces
    has_left, has_right = me > 0, me < n - 1

    load_q = pltpu.make_async_copy(q_hbm, gath.at[me], local_sem.at[0])
    load_c = pltpu.make_async_copy(c_hbm, c_ref, local_sem.at[1])
    load_t = pltpu.make_async_copy(t_hbm, t_ref, local_sem.at[2])
    load_count = pltpu.make_async_copy(count_hbm, count_ref, local_sem.at[3])
    load_q.start()

    barrier = pltpu.get_barrier_semaphore()

    @pl.when(has_left)
    def _():
        pl.semaphore_signal(barrier, inc=1, device_id={"loop": me - 1}, device_id_type=MESH)

    @pl.when(has_right)
    def _():
        pl.semaphore_signal(barrier, inc=1, device_id={"loop": me + 1}, device_id_type=MESH)

    for k in range(1, nf):
        pl.semaphore_signal(
            barrier, inc=1, device_id={"feat": lax.rem(f + k, nf)}, device_id_type=MESH
        )
    load_c.start()
    load_t.start()
    load_count.start()

    def hop(way, block, piece):
        span = gath.at[block, :, pl.ds(pl.multiple_of(piece * cols, 128), cols)]
        return pltpu.make_async_remote_copy(
            src_ref=span,
            dst_ref=span,
            send_sem=send_sem.at[way, block * pieces + piece],
            recv_sem=recv_sem.at[block * pieces + piece],
            device_id={"loop": jnp.clip(me + (2 * way - 1), 0, n - 1)},
            device_id_type=MESH,
        )

    def multiply(block, piece):
        at = pl.ds(pl.multiple_of(piece * cols, 128), cols)
        scaled = (gath[block, :, at].astype(jnp.float32) * inv_ref[:, at]).astype(jnp.bfloat16)
        here = pl.ds(pl.multiple_of(block * q_rows, q_rows), q_rows)
        acc[here, 0:rows] += lax.dot_general(
            scaled, t_ref[:, at], (((1,), (1,)), ((), ())), preferred_element_type=jnp.float32
        )

    acc[...] = jnp.zeros_like(acc)
    load_q.wait()
    pl.semaphore_wait(barrier, has_left.astype(jnp.int32) + has_right.astype(jnp.int32) + nf - 1)

    for piece in range(pieces):
        @pl.when(has_right)
        def _(piece=piece):
            hop(1, me, piece).start()

        @pl.when(has_left)
        def _(piece=piece):
            hop(0, me, piece).start()

    load_c.wait()
    inv_ref[...] = 1.0 / (damping_term + c_ref[...])
    load_t.wait()

    @pl.loop(0, pieces)
    def _(piece):
        multiply(me, piece)

    @pl.loop(0, (n - 1) * pieces)
    def _(step):
        back, piece = step // pieces + 1, lax.rem(step, pieces)
        from_left, from_right = me - back, me + back

        @pl.when(from_left >= 0)
        def _():
            hop(1, from_left, piece).wait_recv()

            @pl.when(has_right)
            def _():
                hop(1, from_left, piece).start()

        @pl.when(from_right < n)
        def _():
            hop(0, from_right, piece).wait_recv()

            @pl.when(has_left)
            def _():
                hop(0, from_right, piece).start()

        @pl.when(from_left >= 0)
        def _():
            multiply(from_left, piece)

        @pl.when(from_right < n)
        def _():
            multiply(from_right, piece)

    turned = acc[...].T
    for k in range(nf):
        part[k] = turned[k * own_rows:(k + 1) * own_rows, 0:part.shape[2]]

    shares = []
    for k in range(1, nf):
        peer = lax.rem(f + k, nf)
        share = pltpu.make_async_remote_copy(
            src_ref=part.at[peer],
            dst_ref=red.at[k - 1],
            send_sem=red_send.at[k - 1],
            recv_sem=red_recv.at[k - 1],
            device_id={"feat": peer},
            device_id_type=MESH,
        )
        share.start()
        shares.append(share)

    @pl.loop(0, n * pieces)
    def _(at):
        block, piece = at // pieces, lax.rem(at, pieces)

        @pl.when(has_right & (block <= me))
        def _():
            hop(1, block, piece).wait_send()

        @pl.when(has_left & (block >= me))
        def _():
            hop(0, block, piece).wait_send()

    load_count.wait()
    slot = f * own_rows + lax.broadcasted_iota(jnp.int32, out_ref.shape, 0)
    total = part[f]
    for k in range(1, nf):
        shares[k - 1].wait_recv()
        total = total + red[k - 1]
    out_ref[...] = jnp.where(slot < count_ref[0], total, 0.0)
    for share in shares:
        share.wait_send()


def on_device(n, nf, train_grads, query_grads, curvature, row_counts):
    rows, width = train_grads.shape
    q_rows = query_grads.shape[0]
    queries = n * q_rows
    pieces = max(1, 16 // n)
    padded = -(-queries // 128) * 128
    lanes = -(-rows // 128) * 128
    hbm = pl.BlockSpec(memory_space=pl.ANY)
    return pl.pallas_call(
        functools.partial(kernel, n, nf, pieces),
        out_shape=jax.ShapeDtypeStruct((rows // nf, queries), jnp.float32),
        in_specs=[hbm] * 4,
        out_specs=pl.BlockSpec(memory_space=pltpu.VMEM),
        scratch_shapes=[
            pltpu.VMEM((n, q_rows, width), jnp.bfloat16),
            pltpu.VMEM((rows, width), jnp.bfloat16),
            pltpu.SMEM((1,), jnp.int32),
            pltpu.VMEM((1, width), jnp.float32),
            pltpu.VMEM((1, width), jnp.float32),
            pltpu.VMEM((padded, lanes), jnp.float32),
            pltpu.VMEM((nf, rows // nf, queries), jnp.float32),
            pltpu.VMEM((nf - 1, rows // nf, queries), jnp.float32),
            pltpu.SemaphoreType.DMA((4,)),
            pltpu.SemaphoreType.DMA((n * pieces,)),
            pltpu.SemaphoreType.DMA((2, n * pieces)),
            pltpu.SemaphoreType.DMA((nf - 1,)),
            pltpu.SemaphoreType.DMA((nf - 1,)),
        ],
        compiler_params=pltpu.CompilerParams(collective_id=0, has_side_effects=True),
    )(train_grads, query_grads, curvature.reshape(1, width), row_counts)


def solution(mesh):
    placed = (
        P(("groups", "loop"), "feat"),
        P(("groups", "loop"), "feat"),
        P("feat"),
        P(("groups", "loop")),
    )
    return jax.shard_map(
        functools.partial(on_device, mesh.shape["loop"], mesh.shape["feat"]),
        mesh=mesh,
        in_specs=placed,
        out_specs=P(("groups", "loop", "feat"), None),
        check_vma=False,
    )
```

time: 68.3 us -> 28.7 us (0.42)
  waiting for transfers between devices: 50.6 us -> 0 us
  Pallas kernels: 0 us -> 26.5 us
  between operations: 14.1 us -> 0.66 us
  matrix products: 1.88 us -> 0 us
  other arithmetic: 0.86 us -> 0 us
    all_gather x1 -> x0, waiting for transfers between devices: 30.8 us -> none  [on_device(): lax.all_gather(query_grads, 'loop', axis=0, tiled=True)]
    pallas_call x0 -> x1, Pallas kernels: none -> 26.5 us  [on_device(): pl.pallas_call(functools.partial(kernel, n, nf, pieces), out_shape=jax.Sh...]
    reduce_scatter x1 -> x0, waiting for transfers between devices: 19 us -> none  [on_device(): lax.psum_scatter(partial_scores, 'feat', scatter_dimension=0, tiled=True)]
    dot_general x1 -> x0, matrix products: 1.88 us -> none  [product(): lax.dot_general(rows, piece, (((1,), (1,)), ((), ())), preferred_element_...]
    add x1 -> x0, other arithmetic: 0.85 us -> none  [scale_rows(): damping_term + curvature[None, :]]
    unnamed x2 -> x0, waiting for transfers between devices: 0.73 us -> none
  transfers between devices with their start and end apart: 2 -> 0, of which waited for: 2 -> 0; matrix products, arithmetic and copies ran while one was open for 1% -> 0% of each run, Pallas kernels for 0% -> 0%
where the time goes in v1:
time: 28.7 us; the launch traced here: 28.5 us
  Pallas kernels  26.5 us (92%)
  local copies, waits for them, and re-layouts  1.3 us (5%)
  between operations  0.66 us (2%)
    pallas_call x1, Pallas kernels, on_device(): pl.pallas_call(functools.partial(kernel, n, nf, pieces), out_shape=jax.Sh...  26.5 us
    unnamed x1, local copies, waits for them, and re-layouts  1.3 us

profile of v1, /device:TPU:0, one launch (start us, length us, event | category | flops | bytes accessed | tf_op | source)
XLA Modules:
  0.0 28.5 jit_solution(1041738274564960397)
XLA Ops:
  0.7 26.5 %shard_map.46 = f32[16,32]{1,0:T(8,128)} custom-call(bf16[64,16384]{1,0:T(8,128)(2,1)} %t_hbm.1, bf16[8,16384]{1,0:T(8,128)(2,1)} %q_hbm.1, f32[1,16384]{1,0:T(1,128)} %bitcast.1, s32[1]{0:T(128)S(6)} %copy.6.count_hbm), custom_call_target="tpu_custom_call" | custom-call | tf_op jit(solution)/shard_map/pallas_call | solution.py:169
  27.2 1.3 %copy.7 = f32[16,32]{1,0:T(8,128)} copy(f32[16,32]{1,0:T(8,128)} %shard_map.46) | data formatting | bytes 4096

commit v2 on v1

v2 whole, which is shorter than its diff:
```python
import functools
import math

import jax
import jax.numpy as jnp
from jax import lax
from jax.experimental import pallas as pl
from jax.experimental.pallas import tpu as pltpu
from jax.sharding import PartitionSpec as P

MESH = pl.DeviceIdType.MESH
damping_term = 0.1


def kernel(
    n, nf, pieces, tail,
    t_hbm, q_hbm, c_hbm, count_hbm, out_ref,
    gath, t_ref, count_ref, c_ref, inv_ref, acc, part, red, t_tail, p_tail, tail_acc, tail_part, tail_red,
    local_sem, recv_sem, send_sem, red_recv, red_send, give_sem, tail_recv, tail_send,
):
    me, f = lax.axis_index("loop"), lax.axis_index("feat")
    rows, width = t_ref.shape
    own_rows = rows // nf
    q_rows = gath.shape[1]
    main = width - tail
    cols = main // pieces
    stride = pieces + 1
    has_left, has_right = me > 0, me < n - 1
    is_end = (me == 0) | (me == n - 1)
    is_helper = (me == 1) | (me == n - 2)

    load_q = pltpu.make_async_copy(q_hbm, gath.at[me], local_sem.at[0])
    load_c = pltpu.make_async_copy(c_hbm, c_ref, local_sem.at[1])
    load_t = pltpu.make_async_copy(t_hbm, t_ref, local_sem.at[2])
    load_count = pltpu.make_async_copy(count_hbm, count_ref, local_sem.at[3])
    load_q.start()

    barrier = pltpu.get_barrier_semaphore()

    @pl.when(has_left)
    def _():
        pl.semaphore_signal(barrier, inc=1, device_id={"loop": me - 1}, device_id_type=MESH)

    @pl.when(has_right)
    def _():
        pl.semaphore_signal(barrier, inc=1, device_id={"loop": me + 1}, device_id_type=MESH)

    for k in range(1, nf):
        pl.semaphore_signal(
            barrier, inc=1, device_id={"feat": lax.rem(f + k, nf)}, device_id_type=MESH
        )
    load_c.start()
    load_t.start()
    load_count.start()

    def columns(piece):
        if piece is None:
            return pl.ds(main, tail)
        return pl.ds(pl.multiple_of(piece * cols, 128), cols)

    def hop(way, block, piece):
        span = gath.at[block, :, columns(piece)]
        at = block * stride + (pieces if piece is None else piece)
        return pltpu.make_async_remote_copy(
            src_ref=span,
            dst_ref=span,
            send_sem=send_sem.at[way, at],
            recv_sem=recv_sem.at[at],
            device_id={"loop": jnp.clip(me + (2 * way - 1), 0, n - 1)},
            device_id_type=MESH,
        )

    def goes_right(piece):
        return has_right if piece is not None else me < n - 2

    def goes_left(piece):
        return has_left if piece is not None else me > 1

    def multiply(block, piece):
        at = columns(piece)
        exact = gath[block, :, at].astype(jnp.float32) * inv_ref[:, at]
        here = pl.ds(pl.multiple_of(block * q_rows, q_rows), q_rows)
        acc[here, 0:rows] += lax.dot_general(
            exact.astype(jnp.bfloat16), t_ref[:, at], (((1,), (1,)), ((), ())),
            preferred_element_type=jnp.float32,
        )
        if piece is None:
            p_tail[here, :] = exact

    def send_own(piece):
        @pl.when(goes_right(piece))
        def _():
            hop(1, me, piece).start()

        @pl.when(goes_left(piece))
        def _():
            hop(0, me, piece).start()

    def arrive(back, piece):
        from_left, from_right = me - back, me + back
        takes_left, takes_right = from_left >= 0, from_right < n
        if piece is None:
            takes_left, takes_right = takes_left & has_right, takes_right & has_left

        @pl.when(takes_left)
        def _():
            hop(1, from_left, piece).wait_recv()

            @pl.when(goes_right(piece))
            def _():
                hop(1, from_left, piece).start()

        @pl.when(takes_right)
        def _():
            hop(0, from_right, piece).wait_recv()

            @pl.when(goes_left(piece))
            def _():
                hop(0, from_right, piece).start()

        @pl.when(takes_left)
        def _():
            multiply(from_left, piece)

        @pl.when(takes_right)
        def _():
            multiply(from_right, piece)

    give = pltpu.make_async_remote_copy(
        src_ref=t_ref.at[:, pl.ds(main, t_tail.shape[1])],
        dst_ref=t_tail,
        send_sem=give_sem.at[0],
        recv_sem=give_sem.at[1],
        device_id={"loop": jnp.where(me == 0, 1, n - 2)},
        device_id_type=MESH,
    ) if tail else None

    acc[...] = jnp.zeros_like(acc)
    load_q.wait()
    pl.semaphore_wait(barrier, has_left.astype(jnp.int32) + has_right.astype(jnp.int32) + nf - 1)

    for piece in range(pieces):
        send_own(piece)
    load_t.wait()
    if tail:
        send_own(None)

        @pl.when(is_end)
        def _():
            give.start()

    load_c.wait()
    inv_ref[...] = 1.0 / (damping_term + c_ref[...])

    @pl.loop(0, pieces)
    def _(piece):
        multiply(me, piece)

    if tail:
        @pl.when(jnp.logical_not(is_end))
        def _():
            multiply(me, None)

    @pl.loop(1, n)
    def _(back):
        @pl.loop(0, pieces)
        def _(piece):
            arrive(back, piece)

        if tail:
            arrive(back, None)

    turned = acc[...].T
    for k in range(nf):
        part[k] = turned[k * own_rows:(k + 1) * own_rows, 0:part.shape[2]]

    shares = []
    for k in range(1, nf):
        peer = lax.rem(f + k, nf)
        share = pltpu.make_async_remote_copy(
            src_ref=part.at[peer],
            dst_ref=red.at[k - 1],
            send_sem=red_send.at[k - 1],
            recv_sem=red_recv.at[k - 1],
            device_id={"feat": peer},
            device_id_type=MESH,
        )
        share.start()
        shares.append(share)

    tail_shares = []
    if tail:
        for k in range(nf):
            peer = lax.rem(f + k, nf)
            tail_shares.append(pltpu.make_async_remote_copy(
                src_ref=tail_part.at[peer],
                dst_ref=tail_red.at[k],
                send_sem=tail_send.at[k],
                recv_sem=tail_recv.at[k],
                device_id={"feat": peer, "loop": jnp.where(me == 1, 0, n - 1)},
                device_id_type=MESH,
            ))

        @pl.when(is_helper)
        def _():
            give.wait_recv()
            tail_acc[...] = jnp.zeros_like(tail_acc)
            wide = math.gcd(tail, 512)

            @pl.loop(0, tail // wide)
            def _(step):
                at = pl.ds(pl.multiple_of(step * wide, 128), wide)
                tail_acc[...] += lax.dot_general(
                    t_tail[:, at], p_tail[:, at].astype(jnp.bfloat16), (((1,), (1,)), ((), ())),
                    preferred_element_type=jnp.float32,
                )

            for k in range(nf):
                tail_part[k] = tail_acc[k * own_rows:(k + 1) * own_rows, :]
            for share in tail_shares:
                share.start()

    @pl.loop(0, n)
    def _(block):
        for piece in [*range(pieces), None][:pieces + (tail > 0)]:
            @pl.when(goes_right(piece) & (block <= me))
            def _():
                hop(1, block, piece).wait_send()

            @pl.when(goes_left(piece) & (block >= me))
            def _():
                hop(0, block, piece).wait_send()

    load_count.wait()
    live = f * own_rows + lax.broadcasted_iota(jnp.int32, out_ref.shape, 0) < count_ref[0]
    total = part[f]
    for k in range(1, nf):
        shares[k - 1].wait_recv()
        total = total + red[k - 1]
    out_ref[...] = jnp.where(live, total, 0.0)
    if tail:
        @pl.when(is_end)
        def _():
            more = jnp.zeros_like(total)
            for k in range(nf):
                tail_shares[k].wait_recv()
                more = more + tail_red[k]
            out_ref[...] = jnp.where(live, total + more, 0.0)
            give.wait_send()

        @pl.when(is_helper)
        def _():
            for share in tail_shares:
                share.wait_send()
    for share in shares:
        share.wait_send()


def on_device(n, nf, train_grads, query_grads, curvature, row_counts):
    rows, width = train_grads.shape
    q_rows = query_grads.shape[0]
    queries = n * q_rows
    pieces = max(1, 16 // n)
    unit = 128 * pieces
    tail = width - width * 26 // 32 // unit * unit if n >= 4 else 0
    padded = -(-queries // 128) * 128
    lanes = -(-rows // 128) * 128
    hbm = pl.BlockSpec(memory_space=pltpu.HBM)
    return pl.pallas_call(
        functools.partial(kernel, n, nf, pieces, tail),
        out_shape=pltpu.VMEM((rows // nf, queries), jnp.float32),
        in_specs=[hbm] * 4,
        out_specs=pl.BlockSpec(memory_space=pltpu.VMEM),
        scratch_shapes=[
            pltpu.VMEM((n, q_rows, width), jnp.bfloat16),
            pltpu.VMEM((rows, width), jnp.bfloat16),
            pltpu.SMEM((1,), jnp.int32),
            pltpu.VMEM((1, width), jnp.float32),
            pltpu.VMEM((1, width), jnp.float32),
            pltpu.VMEM((padded, lanes), jnp.float32),
            pltpu.VMEM((nf, rows // nf, queries), jnp.float32),
            pltpu.VMEM((nf - 1, rows // nf, queries), jnp.float32),
            pltpu.VMEM((rows, tail or 128), jnp.bfloat16),
            pltpu.VMEM((queries, tail or 128), jnp.float32),
            pltpu.VMEM((rows, queries), jnp.float32),
            pltpu.VMEM((nf, rows // nf, queries), jnp.float32),
            pltpu.VMEM((nf, rows // nf, queries), jnp.float32),
            pltpu.SemaphoreType.DMA((4,)),
            pltpu.SemaphoreType.DMA((n * (pieces + 1),)),
            pltpu.SemaphoreType.DMA((2, n * (pieces + 1))),
            pltpu.SemaphoreType.DMA((nf - 1,)),
            pltpu.SemaphoreType.DMA((nf - 1,)),
            pltpu.SemaphoreType.DMA((2,)),
            pltpu.SemaphoreType.DMA((nf,)),
            pltpu.SemaphoreType.DMA((nf,)),
        ],
        compiler_params=pltpu.CompilerParams(collective_id=0, has_side_effects=True),
    )(train_grads, query_grads, curvature.reshape(1, width), row_counts)


def solution(mesh):
    placed = (
        P(("groups", "loop"), "feat"),
        P(("groups", "loop"), "feat"),
        P("feat"),
        P(("groups", "loop")),
    )
    return jax.shard_map(
        functools.partial(on_device, mesh.shape["loop"], mesh.shape["feat"]),
        mesh=mesh,
        in_specs=placed,
        out_specs=P(("groups", "loop", "feat"), None),
        check_vma=False,
    )
```

time: 28.7 us -> 25.4 us (0.89)
  Pallas kernels: 26.5 us -> 23.9 us
  local copies, waits for them, and re-layouts: 1.3 us -> 0.6 us
    pallas_call x1, Pallas kernels: 26.5 us -> 23.9 us  [on_device(): pl.pallas_call(functools.partial(kernel, n, nf, pieces, tail), out_shape=...]
    unnamed x1, local copies, waits for them, and re-layouts: 1.3 us -> 0.6 us
where the time goes in v2:
time: 25.4 us; the launch traced here: 25.2 us
  Pallas kernels  23.9 us (94%)
  between operations  0.66 us (3%)
  local copies, waits for them, and re-layouts  0.6 us (2%)
    pallas_call x1, Pallas kernels, on_device(): pl.pallas_call(functools.partial(kernel, n, nf, pieces, tail), out_shape=...  23.9 us
    unnamed x1, local copies, waits for them, and re-layouts  0.6 us

profile of v2, /device:TPU:0, one launch (start us, length us, event | category | flops | bytes accessed | tf_op | source)
XLA Modules:
  0.0 25.2 jit_solution(2644170785934881429)
XLA Ops:
  0.7 23.9 %shard_map.46 = f32[16,32]{1,0:T(8,128)S(1)} custom-call(bf16[64,16384]{1,0:T(8,128)(2,1)} %t_hbm.1, bf16[8,16384]{1,0:T(8,128)(2,1)} %q_hbm.1, f32[1,16384]{1,0:T(1,128)} %bitcast.1, s32[1]{0:T(128)S(6)} %copy.7.count_hbm), custom_call_target="tpu_custom_call" | custom-call | tf_op jit(solution)/shard_map/pallas_call | solution.py:269
  24.6 0.6 %copy.6 = f32[16,32]{1,0:T(8,128)} copy(f32[16,32]{1,0:T(8,128)S(1)} %shard_map.46) | data formatting | bytes 4096

commit v3 on v2

--- a/solution.py
+++ b/solution.py
@@ -16,7 +16,7 @@
     n, nf, pieces, tail,
     t_hbm, q_hbm, c_hbm, count_hbm, out_ref,
     gath, t_ref, count_ref, c_ref, inv_ref, acc, part, red, t_tail, p_tail, tail_acc, tail_part, tail_red,
-    local_sem, recv_sem, send_sem, red_recv, red_send, give_sem, tail_recv, tail_send,
+    local_sem, recv_sem, send_sem, red_recv, red_send, give_sem, tail_recv, tail_send, ready_sem,
 ):
     me, f = lax.axis_index("loop"), lax.axis_index("feat")
     rows, width = t_ref.shape
@@ -37,10 +37,6 @@
 
     barrier = pltpu.get_barrier_semaphore()
 
-    @pl.when(has_left)
-    def _():
-        pl.semaphore_signal(barrier, inc=1, device_id={"loop": me - 1}, device_id_type=MESH)
-
     @pl.when(has_right)
     def _():
         pl.semaphore_signal(barrier, inc=1, device_id={"loop": me + 1}, device_id_type=MESH)
@@ -77,32 +73,30 @@
         return has_left if piece is not None else me > 1
 
     def multiply(block, piece):
-        at = columns(piece)
-        exact = gath[block, :, at].astype(jnp.float32) * inv_ref[:, at]
+        start, size = (main, tail) if piece is None else (piece * cols, cols)
         here = pl.ds(pl.multiple_of(block * q_rows, q_rows), q_rows)
-        acc[here, 0:rows] += lax.dot_general(
-            exact.astype(jnp.bfloat16), t_ref[:, at], (((1,), (1,)), ((), ())),
-            preferred_element_type=jnp.float32,
-        )
-        if piece is None:
-            p_tail[here, :] = exact
-
-    def send_own(piece):
-        @pl.when(goes_right(piece))
-        def _():
-            hop(1, me, piece).start()
-
-        @pl.when(goes_left(piece))
-        def _():
-            hop(0, me, piece).start()
+        wide = size // 2 if size % 256 == 0 else size
+
+        @pl.loop(0, size // wide)
+        def _(step):
+            at = pl.ds(pl.multiple_of(start + step * wide, 128), wide)
+            exact = gath[block, :, at].astype(jnp.float32) * inv_ref[:, at]
+            acc[here, 0:rows] += lax.dot_general(
+                exact.astype(jnp.bfloat16), t_ref[:, at], (((1,), (1,)), ((), ())),
+                preferred_element_type=jnp.float32,
+            )
+            if piece is None:
+                p_tail[here, pl.ds(pl.multiple_of(step * wide, 128), wide)] = exact
 
     def arrive(back, piece):
         from_left, from_right = me - back, me + back
         takes_left, takes_right = from_left >= 0, from_right < n
         if piece is None:
-            takes_left, takes_right = takes_left & has_right, takes_right & has_left
-
-        @pl.when(takes_left)
+            inner = jnp.logical_not(is_end)
+            takes_left, takes_right = takes_left & inner, takes_right & inner
+        moved = back > 0
+
+        @pl.when(takes_left & moved)
         def _():
             hop(1, from_left, piece).wait_recv()
 
@@ -110,7 +104,7 @@
             def _():
                 hop(1, from_left, piece).start()
 
-        @pl.when(takes_right)
+        @pl.when(takes_right & moved)
         def _():
             hop(0, from_right, piece).wait_recv()
 
@@ -118,13 +112,11 @@
             def _():
                 hop(0, from_right, piece).start()
 
-        @pl.when(takes_left)
-        def _():
-            multiply(from_left, piece)
-
-        @pl.when(takes_right)
-        def _():
-            multiply(from_right, piece)
+        @pl.loop(0, 2)
+        def _(side):
+            @pl.when(((side == 0) & takes_left) | ((side == 1) & takes_right & moved))
+            def _():
+                multiply(me + (2 * side - 1) * back, piece)
 
     give = pltpu.make_async_remote_copy(
         src_ref=t_ref.at[:, pl.ds(main, t_tail.shape[1])],
@@ -137,14 +129,36 @@
 
     acc[...] = jnp.zeros_like(acc)
     load_q.wait()
-    pl.semaphore_wait(barrier, has_left.astype(jnp.int32) + has_right.astype(jnp.int32) + nf - 1)
-
-    for piece in range(pieces):
-        send_own(piece)
+    pl.semaphore_wait(barrier, has_left.astype(jnp.int32) + nf - 1)
+
+    @pl.when(has_left)
+    def _():
+        pl.semaphore_signal(ready_sem, inc=1, device_id={"loop": me - 1}, device_id_type=MESH)
+
+        @pl.loop(0, pieces)
+        def _(piece):
+            hop(0, me, piece).start()
+
+    if tail:
+        @pl.when(goes_left(None))
+        def _():
+            hop(0, me, None).start()
+
+    @pl.when(has_right)
+    def _():
+        pl.semaphore_wait(ready_sem, 1)
+
+        @pl.loop(0, pieces)
+        def _(piece):
+            hop(1, me, piece).start()
+
+    if tail:
+        @pl.when(goes_right(None))
+        def _():
+            hop(1, me, None).start()
+
     load_t.wait()
     if tail:
-        send_own(None)
-
         @pl.when(is_end)
         def _():
             give.start()
@@ -152,16 +166,7 @@
     load_c.wait()
     inv_ref[...] = 1.0 / (damping_term + c_ref[...])
 
-    @pl.loop(0, pieces)
-    def _(piece):
-        multiply(me, piece)
-
-    if tail:
-        @pl.when(jnp.logical_not(is_end))
-        def _():
-            multiply(me, None)
-
-    @pl.loop(1, n)
+    @pl.loop(0, n)
     def _(back):
         @pl.loop(0, pieces)
         def _(piece):
@@ -222,7 +227,7 @@
 
     @pl.loop(0, n)
     def _(block):
-        for piece in [*range(pieces), None][:pieces + (tail > 0)]:
+        def sent(piece):
             @pl.when(goes_right(piece) & (block <= me))
             def _():
                 hop(1, block, piece).wait_send()
@@ -230,6 +235,13 @@
             @pl.when(goes_left(piece) & (block >= me))
             def _():
                 hop(0, block, piece).wait_send()
+
+        @pl.loop(0, pieces)
+        def _(piece):
+            sent(piece)
+
+        if tail:
+            sent(None)
 
     load_count.wait()
     live = f * own_rows + lax.broadcasted_iota(jnp.int32, out_ref.shape, 0) < count_ref[0]
@@ -262,7 +274,7 @@
     queries = n * q_rows
     pieces = max(1, 16 // n)
     unit = 128 * pieces
-    tail = width - width * 26 // 32 // unit * unit if n >= 4 else 0
+    tail = width - width * 27 // 32 // unit * unit if n >= 4 else 0
     padded = -(-queries // 128) * 128
     lanes = -(-rows // 128) * 128
     hbm = pl.BlockSpec(memory_space=pltpu.HBM)
@@ -293,6 +305,7 @@
             pltpu.SemaphoreType.DMA((2,)),
             pltpu.SemaphoreType.DMA((nf,)),
             pltpu.SemaphoreType.DMA((nf,)),
+            pltpu.SemaphoreType.REGULAR,
         ],
         compiler_params=pltpu.CompilerParams(collective_id=0, has_side_effects=True),
     )(train_grads, query_grads, curvature.reshape(1, width), row_counts)

time: 25.4 us -> 24.9 us (0.980)
  Pallas kernels: 23.9 us -> 23.5 us
    pallas_call x1, Pallas kernels: 23.9 us -> 23.5 us  [on_device(): pl.pallas_call(functools.partial(kernel, n, nf, pieces, tail), out_shape=...]
where the time goes in v3:
time: 24.9 us; the launch traced here: 24.8 us
  Pallas kernels  23.5 us (94%)
  between operations  0.66 us (3%)
  local copies, waits for them, and re-layouts  0.6 us (2%)
    pallas_call x1, Pallas kernels, on_device(): pl.pallas_call(functools.partial(kernel, n, nf, pieces, tail), out_shape=...  23.5 us
    unnamed x1, local copies, waits for them, and re-layouts  0.6 us

profile of v3, /device:TPU:0, one launch (start us, length us, event | category | flops | bytes accessed | tf_op | source)
XLA Modules:
  0.0 24.8 jit_solution(17021526526071282909)
XLA Ops:
  0.7 23.5 %shard_map.46 = f32[16,32]{1,0:T(8,128)S(1)} custom-call(bf16[64,16384]{1,0:T(8,128)(2,1)} %t_hbm.1, bf16[8,16384]{1,0:T(8,128)(2,1)} %q_hbm.1, f32[1,16384]{1,0:T(1,128)} %bitcast.1, s32[1]{0:T(128)S(6)} %copy.7.count_hbm), custom_call_target="tpu_custom_call" | custom-call | tf_op jit(solution)/shard_map/pallas_call | solution.py:281
  24.2 0.6 %copy.6 = f32[16,32]{1,0:T(8,128)} copy(f32[16,32]{1,0:T(8,128)S(1)} %shard_map.46) | data formatting | bytes 4096

commit v4 on v3

--- a/solution.py
+++ b/solution.py
@@ -96,6 +96,14 @@
             takes_left, takes_right = takes_left & inner, takes_right & inner
         moved = back > 0
 
+        @pl.when(takes_right & moved)
+        def _():
+            hop(0, from_right, piece).wait_recv()
+
+            @pl.when(goes_left(piece))
+            def _():
+                hop(0, from_right, piece).start()
+
         @pl.when(takes_left & moved)
         def _():
             hop(1, from_left, piece).wait_recv()
@@ -103,14 +111,6 @@
             @pl.when(goes_right(piece))
             def _():
                 hop(1, from_left, piece).start()
-
-        @pl.when(takes_right & moved)
-        def _():
-            hop(0, from_right, piece).wait_recv()
-
-            @pl.when(goes_left(piece))
-            def _():
-                hop(0, from_right, piece).start()
 
         @pl.loop(0, 2)
         def _(side):

time: 24.9 us -> 24.9 us (level)
  no operation moved by 1% of the time
where the time goes in v4:
time: 24.9 us; the launch traced here: 24.8 us
  Pallas kernels  23.5 us (94%)
  between operations  0.66 us (3%)
  local copies, waits for them, and re-layouts  0.6 us (2%)
    pallas_call x1, Pallas kernels, on_device(): pl.pallas_call(functools.partial(kernel, n, nf, pieces, tail), out_shape=...  23.5 us
    unnamed x1, local copies, waits for them, and re-layouts  0.6 us

profile of v4, /device:TPU:0, one launch (start us, length us, event | category | flops | bytes accessed | tf_op | source)
XLA Modules:
  0.0 24.8 jit_solution(3402662134195770022)
XLA Ops:
  0.7 23.5 %shard_map.46 = f32[16,32]{1,0:T(8,128)S(1)} custom-call(bf16[64,16384]{1,0:T(8,128)(2,1)} %t_hbm.1, bf16[8,16384]{1,0:T(8,128)(2,1)} %q_hbm.1, f32[1,16384]{1,0:T(1,128)} %bitcast.1, s32[1]{0:T(128)S(6)} %copy.7.count_hbm), custom_call_target="tpu_custom_call" | custom-call | tf_op jit(solution)/shard_map/pallas_call | solution.py:281
  24.2 0.6 %copy.6 = f32[16,32]{1,0:T(8,128)} copy(f32[16,32]{1,0:T(8,128)S(1)} %shard_map.46) | data formatting | bytes 4096
